TPU v7x, 16 devices: a 4x2x1 block of a 4x4x8 slice. The times are simulated.
16 devices in a mesh: dp: 2 (over y, z), ep: 8 (over x, core).
Axes of the slice: x: 4, y: 2, z: 1, core: 2. Of those that a mesh axis runs over, the one named last changes fastest.
The devices are a block of a 4x4x8 slice.
Arguments:
- x: bfloat16 [2, 8, 256, 4096], P('dp', 'ep'), parts along dimension 0
- expert: int32 [2, 8, 256, 8], P('dp', 'ep'), parts along dimension 0
- slot: int32 [2, 8, 256, 8], P('dp', 'ep'), parts along dimension 0
- gate: float32 [2, 8, 256, 8], P('dp', 'ep'), parts along dimension 0
- w_gate: bfloat16 [64, 4096, 1408], P('ep')
- w_up: bfloat16 [64, 4096, 1408], P('ep')
- w_down: bfloat16 [64, 1408, 4096], P('ep')
- s_gate: bfloat16 [4096, 1408], replicated
- s_up: bfloat16 [4096, 1408], replicated
- s_down: bfloat16 [1408, 4096], replicated
Outputs:
- y: bfloat16 [2, 8, 256, 4096], P('dp', 'ep'), parts along dimension 0
There are 2 independent parts. A program takes and returns all parts, laid end to end along the dimension named above; an argument that names none is the same for every part.
All inputs are finite; a program needn't handle non-finite values.
Results may differ from a plain program's by a relative error of at most 0.009.
Values are sent between devices in bfloat16 or wider.
A program may use at most 768 MiB of HBM per device.

v0:
```python
import jax
import jax.numpy as jnp
from jax import lax
from jax.sharding import NamedSharding, PartitionSpec as P


def einsum(form, a, b):
    return jnp.einsum(form, a.astype(jnp.float32), b.astype(jnp.float32))


def for_all(x, s_gate, s_up, s_down):
    h = jax.nn.silu(einsum("...d,df->...f", x, s_gate)) * einsum("...d,df->...f", x, s_up)
    return einsum("...f,fd->...d", h.astype(jnp.bfloat16), s_down)


def solution(mesh):
    def placed(v, *spec):
        return lax.with_sharding_constraint(v, NamedSharding(mesh, P(*spec)))

    def step(x, expert, slot, gate, w_gate, w_up, w_down, s_gate, s_up, s_down):
        experts, (tokens, top) = w_gate.shape[0], expert.shape[2:]
        slots = 5 * tokens * top // (4 * experts)
        to_expert = jax.nn.one_hot(expert, experts, dtype=jnp.bfloat16)
        to_slot = jax.nn.one_hot(slot, slots, dtype=jnp.bfloat16)
        weighted = to_expert * gate[..., None].astype(jnp.bfloat16)
        dispatch = einsum("abtke,abtkc->abtec", to_expert, to_slot).astype(jnp.bfloat16)
        combine = einsum("abtke,abtkc->abtec", weighted, to_slot).astype(jnp.bfloat16)
        z = einsum("abtec,abtd->aebcd", dispatch, x).astype(jnp.bfloat16)
        z = placed(z, "dp", None, "ep", None, None)
        z = placed(z, "dp", "ep", None, None, None)
        h = jax.nn.silu(einsum("aebcd,edf->aebcf", z, w_gate))
        h = (h * einsum("aebcd,edf->aebcf", z, w_up)).astype(jnp.bfloat16)
        out = einsum("aebcf,efd->aebcd", h, w_down).astype(jnp.bfloat16)
        out = placed(out, "dp", "ep", None, None, None)
        out = placed(out, "dp", None, "ep", None, None)
        y = einsum("abtec,aebcd->abtd", combine, out)
        return (y + for_all(x, s_gate, s_up, s_down)).astype(jnp.bfloat16)

    return step
```

profile of v0, /device:TPU:112, one launch (start us, length us, event | category | flops | bytes accessed | tf_op | source)
XLA Modules:
  0.0 676.2 jit_solution(11651452063975697959)
XLA Ops:
  0.0 0.0 copy-start
  0.0 1.0 copy.10
  1.0 0.0 copy-start.1
  1.0 0.8 copy.12
  1.8 0.0 copy-done.1
  1.8 0.0 copy-start.3
  1.9 0.6 copy-done.3
  2.5 3.6 convolution_convert_fusion.1
  6.1 5.6 copy.13
  11.8 0.0 copy-done
  11.8 9.9 %convolution_convert_fusion = bf16[64,40,4096]{2,1,0:T(8,128)(2,1)} fusion(bf16[256,64,40]{0,2,1:T(8,128)(2,1)S(1)} %copy.13, bf16[1,1,256,4096]{3,2,1,0:T(8,128)(2,1)S(1)} %copy-done), kind=kOutput, calls=%fused_computation.18 | convolution fusion | flops 5379194880 | bytes 24379392 | tf_op jit(solution)/abtec,abtd->aebcd/dot_general | solution.py:8
  21.7 238.1 %all-to-all.4 = bf16[1,8,8,1,40,4096]{5,4,2,3,0,1:T(8,128)(2,1)} all-to-all(bf16[1,8,8,1,40,4096]{5,4,2,3,0,1:T(8,128)(2,1)} %bitcast.115), channel_id=1, replica_groups=mesh['dp'=2,'ep'=8] {'ep'}, dimensions={1} | all-to-all | bytes 41943040 | tf_op jit(solution)/sharding_constraint;jit(solution)/sharding_constraint | solution.py:18
  259.8 50.2 %fusion.4 = f32[8,8,40,1408]{3,2,1,0:T(8,128)} fusion(bf16[8,4096,1408]{2,1,0:T(8,128)(2,1)} %param.4, bf16[1,8,8,1,40,4096]{5,4,2,3,0,1:T(8,128)(2,1)} %all-to-all.4), kind=kOutput, calls=%fused_computation.4 | convolution fusion | flops 29527900160 | bytes 127664128 | tf_op jit(solution)/aebcd,edf->aebcf/dot_general | solution.py:8
  310.0 49.7 %fusion.10 = bf16[1,8,8,40,1408]{4,3,2,1,0:T(8,128)(2,1)} fusion(f32[8,8,40,1408]{3,2,1,0:T(8,128)} %fusion.4, bf16[8,4096,1408]{2,1,0:T(8,128)(2,1)} %param.5, bf16[1,8,8,1,40,4096]{5,4,2,3,0,1:T(8,128)(2,1)} %all-to-all.4), kind=kOutput, calls=%fused_computation.12 | convolution fusion | flops 29549527040 | bytes 134873088 | tf_op jit(solution)/aebcd,edf->aebcf/dot_general | solution.py:8
  359.7 48.9 %convert_bitcast_fusion = bf16[1,8,8,1,40,4096]{5,4,2,1,3,0:T(8,128)(2,1)} fusion(bf16[8,1408,4096]{2,1,0:T(8,128)(2,1)} %param.6, bf16[1,8,8,40,1408]{4,3,2,1,0:T(8,128)(2,1)} %fusion.10), kind=kOutput, calls=%fused_computation.8 | convolution fusion | flops 29538385920 | bytes 120455168 | tf_op jit(solution)/aebcf,efd->aebcd/dot_general | solution.py:8
  408.6 17.5 %copy.16 = bf16[1,8,8,1,40,4096]{5,4,1,3,0,2:T(8,128)(2,1)} copy(bf16[1,8,8,1,40,4096]{5,4,2,1,3,0:T(8,128)(2,1)} %convert_bitcast_fusion) | data formatting | bytes 41943040 | tf_op jit(solution)/sharding_constraint;jit(solution)/sharding_constraint | solution.py:18
  426.1 0.0 copy-start.5
  426.1 0.0 copy-start.2
  426.1 0.0 copy-start.4
  426.1 6.7 all-to-all-start.1
  432.8 0.0 copy-done.5
  432.8 0.1 copy.11
  433.0 0.0 copy-done.2
  433.0 0.0 copy-done.4
  433.0 4.3 convolution_convert_fusion.2
  437.3 5.6 copy.23
  442.9 7.3 %convolution_bitcast_fusion.2 = f32[1,1,256,1408]{3,2,1,0:T(8,128)} fusion(bf16[4096,1408]{1,0:T(8,128)(2,1)} %param.7, bf16[1,1,256,4096]{3,2,1,0:T(8,128)(2,1)S(1)} %copy-done), kind=kOutput, calls=%fused_computation.26 | convolution fusion | flops 2952790016 | bytes 15073280 | tf_op jit(solution)/...d,df->...f/dot_general | solution.py:8
  450.2 16.7 %fusion.37 = f32[256,4096]{1,0:T(8,128)} fusion(bf16[1408,4096]{1,0:T(8,128)(2,1)} %param.9, bf16[4096,1408]{1,0:T(8,128)(2,1)} %param.8, bf16[1,1,256,4096]{3,2,1,0:T(8,128)(2,1)S(1)} %copy-done, f32[1,1,256,1408]{3,2,1,0:T(8,128)} %convolution_bitcast_fusion.2), kind=kOutput, calls=%fused_computation.39 | convolution fusion | flops 5907742720 | bytes 30801920 | tf_op jit(solution)/...f,fd->...d/dot_general | solution.py:8
  466.9 194.9 %all-to-all-done.1 = bf16[1,8,8,1,40,4096]{5,4,1,3,0,2:T(8,128)(2,1)} async-done(((bf16[1,8,8,1,40,4096]{5,4,1,3,0,2:T(8,128)(2,1)}), bf16[1,8,8,1,40,4096]{5,4,1,3,0,2:T(8,128)(2,1)}, u32[]{:S(2)}, u32[]{:S(2)}) %all-to-all-start.1) | async-done | bytes 20971552 | tf_op jit(solution)/sharding_constraint;jit(solution)/sharding_constraint | solution.py:18
  661.8 14.4 %fusion.23 = bf16[1,1,256,4096]{3,2,1,0:T(8,128)(2,1)} fusion(f32[256,4096]{1,0:T(8,128)} %fusion.37, bf16[256,64,40]{0,2,1:T(8,128)(2,1)S(1)} %copy.23, bf16[64,40,4096]{2,1,0:T(8,128)(2,1)} %bitcast.25), kind=kOutput, calls=%fused_computation.23 | convolution fusion | flops 5370806272 | bytes 28573696 | tf_op jit(solution)/abtec,aebcd->abtd/dot_general | solution.py:8
  (1 shorter events, 0.0 us)
Async XLA Ops:
  0.0 11.8 %copy-start = (bf16[1,1,256,4096]{3,2,1,0:T(8,128)(2,1)S(1)}, bf16[1,1,256,4096]{3,2,1,0:T(8,128)(2,1)}, u32[]{:S(2)}) copy-start(bf16[1,1,256,4096]{3,2,1,0:T(8,128)(2,1)} %param.3) | copy-start | bytes 6291460
  1.0 0.9 copy-start.1
  1.8 0.7 copy-start.3
  426.1 6.7 copy-start.5
  426.1 6.8 %copy-start.2 = (s32[256,8]{1,0:T(8,128)S(1)}, s32[256,8]{1,0:T(8,128)}, u32[]{:S(2)}) copy-start(s32[256,8]{1,0:T(8,128)} %copy-done.1) | copy-start | bytes 24580
  426.1 6.8 %copy-start.4 = (s32[256,8]{1,0:T(8,128)S(1)}, s32[256,8]{1,0:T(8,128)}, u32[]{:S(2)}) copy-start(s32[256,8]{1,0:T(8,128)} %copy-done.3) | copy-start | bytes 24580
  426.1 235.7 %all-to-all-start.1 = ((bf16[1,8,8,1,40,4096]{5,4,1,3,0,2:T(8,128)(2,1)}), bf16[1,8,8,1,40,4096]{5,4,1,3,0,2:T(8,128)(2,1)}, u32[]{:S(2)}, u32[]{:S(2)}) async-start(bf16[1,8,8,1,40,4096]{5,4,1,3,0,2:T(8,128)(2,1)} %copy.16), calls=%async_computation.1 | async-start | bytes 41943040 | tf_op jit(solution)/sharding_constraint;jit(solution)/sharding_constraint | solution.py:18
where the time goes:
time: 677 us; the launch traced here: 676 us
  blocking collectives  238 us (35%)
  matrix products  205 us (30%)
  waiting for transfers between devices  195 us (29%)
  local copies, waits for them, and re-layouts  31.3 us (5%)
    another operation x1, blocking collectives, placed(): return lax.with_sharding_constraint(v, NamedSharding(mesh, P(*spec)))  238 us
    dot_general x9, matrix products, einsum(): return jnp.einsum(form, a.astype(jnp.float32), b.astype(jnp.float32))  205 us
    another operation x1, waiting for transfers between devices, placed(): return lax.with_sharding_constraint(v, NamedSharding(mesh, P(*spec)))  195 us
    another operation x1, local copies, waits for them, and re-layouts, placed(): return lax.with_sharding_constraint(v, NamedSharding(mesh, P(*spec)))  17.5 us
  transfers between devices with their start and end apart: 1, of which 1 were waited for; matrix products, arithmetic and copies ran while one was open for 5% of the time, Pallas kernels for 0%

commit v1 on v0

v1 whole, which is shorter than its diff:
```python
import functools

import jax
import jax.numpy as jnp
from jax import lax
from jax.experimental import pallas as pl
from jax.experimental.pallas import tpu as pltpu
from jax.sharding import PartitionSpec as P

MESH = pl.DeviceIdType.MESH
BF, F32 = jnp.bfloat16, jnp.float32
ANY = pl.BlockSpec(memory_space=pl.ANY)
VM = pl.BlockSpec(memory_space=pltpu.VMEM)
W = 512
NT = 256


def dot(a, b):
    return jnp.dot(a, b, preferred_element_type=F32)


def remote(src, dst, send, recv, to):
    return pltpu.make_async_remote_copy(
        src_ref=src, dst_ref=dst, send_sem=send, recv_sem=recv,
        device_id={"ep": to}, device_id_type=MESH,
    )


def places():
    me = lax.axis_index("ep")
    chip, core = me // 2, me % 2
    at = lambda step: ((chip + step) % 4) * 2 + core
    return me, chip, core, chip * 2 + 1 - core, at(1), at(3), at(2)


def greet(n, me):
    barrier = pltpu.get_barrier_semaphore()
    for off in range(1, n):
        pl.semaphore_signal(barrier, inc=1, device_id={"ep": (me + off) % n}, device_id_type=MESH)
    pl.semaphore_wait(barrier, n - 1)


def project(n, slots, x, rt, sg, su, wg, wu, h_out, hs_out, rt_all,
            xg, oh, acc, wbuf, zf, z, hst, lsem, wsem, hsem, rts, rtr, own_s, own_r, fwd_s, fwd_r, par_s, par_r):
    per, _, ff = wg.shape
    T, D = x.shape
    half, rows, chunks = T // 2, n * slots, D // W
    me, chip, core, partner, right, left, opp = places()
    mine = per * slots

    def tile_copies(g, e, slot):
        return (
            pltpu.make_async_copy(wg.at[e, pl.ds(g * W, W), :], wbuf.at[slot, :, pl.ds(0, ff)], wsem.at[slot, 0]),
            pltpu.make_async_copy(wu.at[e, pl.ds(g * W, W), :], wbuf.at[slot, :, pl.ds(ff, ff)], wsem.at[slot, 1]),
        )

    def shared_copies(g, slot):
        return (
            pltpu.make_async_copy(sg.at[pl.ds(g * W, W), :], wbuf.at[slot, :, pl.ds(0, ff)], wsem.at[slot, 0]),
            pltpu.make_async_copy(su.at[pl.ds(g * W, W), :], wbuf.at[slot, :, pl.ds(ff, ff)], wsem.at[slot, 1]),
        )

    def fetch(t):
        slot = t % 3

        @pl.when(t < chunks)
        def _():
            for c in shared_copies(t, slot):
                c.start()

        @pl.when((t >= chunks) & (t < chunks + chunks * per))
        def _():
            for c in tile_copies((t - chunks) // per, (t - chunks) % per, slot):
                c.start()

    def arrived(t):
        for c in shared_copies(0, t % 3):
            c.wait()

    def local(k):
        return pltpu.make_async_copy(x.at[:, pl.ds(k * W, W)], xg.at[k, me], lsem.at[k])

    fetch(0)
    for k in range(chunks):
        local(k).start()
    fetch(1)

    A, B = pl.ds(0, half), pl.ds(half, half)

    def own(k, way, part):
        ref = xg.at[k, me, (A, B)[part]]
        return remote(ref, ref, own_s.at[way, part, k], own_r.at[way, part, k], (right, left)[way])

    def fwd(k, way):
        ref = xg.at[k, (left, right)[way], (A, B)[way]]
        return remote(ref, ref, fwd_s.at[way, k], fwd_r.at[way, k], (right, left)[way])

    def par(k, i):
        ref = (xg.at[k, me], xg.at[k, left], xg.at[k, right], xg.at[k, opp, A], xg.at[k, opp, B])[i]
        return remote(ref, ref, par_s.at[i, k], par_r.at[i, k], partner)

    def send_own(k):
        own(k, 0, 0).start()
        own(k, 1, 1).start()
        own(k, 0, 1).start()
        own(k, 1, 0).start()
        par(k, 0).start()

    rt_all[me] = rt[...]
    greet(n, me)
    local(0).wait()
    send_own(0)
    for off in range(1, n):
        remote(rt, rt_all.at[me], rts.at[off], rtr.at[off], (me + off) % n).start()

    def near(k):
        own(k, 0, 0).wait_recv()
        fwd(k, 0).start()
        own(k, 1, 1).wait_recv()
        fwd(k, 1).start()

        @pl.when(k + 1 < chunks)
        def _():
            send_own(k + 1)

        own(k, 0, 1).wait_recv()
        par(k, 1).start()
        own(k, 1, 0).wait_recv()
        par(k, 2).start()

    def far(k):
        fwd(k, 0).wait_recv()
        par(k, 3).start()
        fwd(k, 1).wait_recv()
        par(k, 4).start()

    def service(g, e):
        @pl.when((e == 4) & (g < chunks))
        def _():
            near(g)

        @pl.when((e == per - 1) & (g < chunks))
        def _():
            far(g)

    def gate_up(e, lhs, slot, first, n_rows):
        width = 2 * ff
        for c in range(0, width, NT):
            cols = pl.ds(c, min(NT, width - c))
            old = acc[e, pl.ds(0, n_rows), cols]
            acc[e, pl.ds(0, n_rows), cols] = jnp.where(first, 0.0, old) + dot(lhs, wbuf[slot, :, cols])

    def act(e, hslot, n_rows):
        step = 32

        @pl.loop(0, n_rows // step)
        def _(r):
            at = pl.ds(pl.multiple_of(r * step, step), step)
            g = acc[e, at, pl.ds(0, ff)]
            u = acc[e, at, pl.ds(ff, ff)]
            hst[hslot, at, :] = (jax.nn.silu(g) * u).astype(BF)

    def shared_out():
        return pltpu.make_async_copy(hst.at[0, pl.ds(0, T)], hs_out, hsem.at[0])

    def expert_out(e):
        return pltpu.make_async_copy(hst.at[e % 2], h_out.at[e], hsem.at[e % 2])

    @pl.loop(0, chunks)
    def _(t):
        arrived(t)
        fetch(t + 2)

        @pl.when(t > 0)
        def _():
            local(t).wait()

        gate_up(0, xg[t, me], t % 3, t == 0, T)
        service(0, t)

    act(0, 0, T)
    shared_out().start()

    for off in range(1, n):
        remote(rt, rt_all.at[me], rts.at[off], rtr.at[off], (me + off) % n).wait()

    @pl.loop(0, n)
    def _(b):
        row = lax.broadcasted_iota(jnp.int32, (mine, T), 0).astype(F32) + (me * mine).astype(F32)
        codes = rt_all[b]
        hit = jnp.zeros((mine, T), F32)
        for j in range(codes.shape[0] // 2):
            hit = jnp.where(codes[j:j + 1, :] == row, 1.0, hit)
        oh[b] = hit.astype(BF)

    @pl.loop(0, chunks)
    def _(k):
        for i in range(5):
            par(k, i).wait_recv()

        @pl.loop(0, n // 2)
        def _(p):
            for i in range(2):
                b = p * 2 + i
                for c in range(0, W, NT):
                    zf[i, :, pl.ds(c, NT)] = dot(oh[b], xg[k, b, :, pl.ds(c, NT)])
            at = pl.ds(pl.multiple_of(p * 2 * slots, 16), 2 * slots)
            for e in range(per):
                lines = pl.ds(e * slots, slots)
                z[e, at, :] = jnp.concatenate([zf[0, lines, :], zf[1, lines, :]], axis=0).astype(BF)

        @pl.loop(0, per)
        def _(e):
            t = chunks + k * per + e
            arrived(t)
            fetch(t + 2)
            gate_up(e, z[e], t % 3, k == 0, rows)
            service(k + 1, e)

            @pl.when(k == chunks - 1)
            def _():
                @pl.when(e == 0)
                def _():
                    shared_out().wait()

                @pl.when(e >= 2)
                def _():
                    expert_out(e - 2).wait()

                act(e, e % 2, rows)
                expert_out(e).start()

    expert_out(per - 2).wait()
    expert_out(per - 1).wait()

    @pl.loop(0, chunks)
    def _(k):
        for way in range(2):
            own(k, way, 0).wait_send()
            own(k, way, 1).wait_send()
            fwd(k, way).wait_send()
        for i in range(5):
            par(k, i).wait_send()


def finish(n, slots, h, hs, rt_all, wd, sd, y,
           hv, hsv, cm, wbuf, of, o, keep, psend, precv, tot, s3, s1s, s1r, s3s, s3r, yb,
           hsem, wsem, ysem, par_s, par_r, s1_s, s1_r, s3_s, s3_r):
    per, ff, D = wd.shape
    T = hs.shape[0]
    half, chunks = T // 2, D // W
    me, chip, core, partner, right, left, opp = places()
    mine = per * slots
    steps = per + 1
    A, B = pl.ds(0, half), pl.ds(half, half)
    parts = (A, B)
    depth = wbuf.shape[0]

    def expert_tile(k, e, slot):
        return pltpu.make_async_copy(wd.at[e, :, pl.ds(k * W, W)], wbuf.at[slot], wsem.at[slot])

    def shared_tile(k, slot):
        return pltpu.make_async_copy(sd.at[:, pl.ds(k * W, W)], wbuf.at[slot], wsem.at[slot])

    def fetch(t):
        slot, k, i = t % depth, t // steps, t % steps

        @pl.when((t < chunks * steps) & (i < per))
        def _():
            expert_tile(k, i, slot).start()

        @pl.when((t < chunks * steps) & (i == per))
        def _():
            shared_tile(k, slot).start()

    def arrived(t):
        shared_tile(0, t % depth).wait()

    def load(e):
        return pltpu.make_async_copy(h.at[e], hv.at[e], hsem.at[e])

    load_s = pltpu.make_async_copy(hs, hsv, hsem.at[per])
    load(0).start()
    fetch(0)
    load(1).start()
    fetch(1)
    for e in range(2, per):
        load(e).start()
    load_s.start()
    for t in range(2, depth - 1):
        fetch(t)

    pad = o.shape[1]

    @pl.loop(0, n)
    def _(b):
        at = lax.broadcasted_iota(jnp.int32, (pad, T), 0)
        row = jnp.where(at < mine, at + me * mine, -2).astype(F32)
        table = rt_all[b]
        top = table.shape[0] // 2
        got = jnp.zeros((pad, T), F32)
        for j in range(top):
            got = jnp.where(table[j:j + 1, :] == row, table[top + j:top + j + 1, :], got)
        cm[b] = got.T.astype(BF)
        o[b, pl.ds(mine, pad - mine), :] = jnp.zeros((pad - mine, W), BF)

    greet(n, me)

    def pair(k):
        return remote(psend.at[k % 2], precv.at[k], par_s.at[k], par_r.at[k], partner)

    def first(k, way):
        return remote(s1s.at[k, way], s1r.at[k, way], s1_s.at[way, k], s1_r.at[way, k], (right, left)[way])

    def second(k, way, part):
        return remote(s3s.at[k, way, parts[part]], s3r.at[k, way, parts[part]],
                      s3_s.at[way, part, k], s3_r.at[way, part, k], (right, left)[way])

    def chip_sums(k):
        pair(k).wait_recv()
        cols = pl.ds(pl.multiple_of(k * W, W), W)

        def both(step, part):
            c = (chip + step) % 4
            return keep[c, parts[part], :] + precv[k, c, parts[part], :].astype(F32)

        for way in range(2):
            s1s[k, way] = both(2, way).astype(BF)
            first(k, way).start()
        for way in range(2):
            far = 1 - way
            s3s[k, way, parts[far], :] = both((1, 3)[way], far).astype(BF)
            second(k, way, far).start()
        for way in range(2):
            s3[k, way] = both((1, 3)[way], way)
        for part in range(2):
            tot[parts[part], cols] = tot[parts[part], cols] + both(0, part)

    def pass_on(k):
        for way in range(2):
            first(k, way).wait_recv()
            s3s[k, way, parts[way], :] = (s3[k, way] + s1r[k, way].astype(F32)).astype(BF)
            second(k, way, way).start()

    def out(k):
        return pltpu.make_async_copy(yb.at[k % 2], y.at[:, pl.ds(k * W, W)], ysem.at[k % 2])

    def complete(k):
        for way in range(2):
            for part in range(2):
                second(k, way, part).wait_recv()

        @pl.when(k >= 2)
        def _():
            out(k - 2).wait()

        cols = pl.ds(pl.multiple_of(k * W, W), W)
        yb[k % 2] = (tot[:, cols] + s3r[k, 0].astype(F32) + s3r[k, 1].astype(F32)).astype(BF)
        out(k).start()

    @pl.loop(0, chunks)
    def _(k):
        @pl.loop(0, per // 2)
        def _(p):
            for i in range(2):
                e = p * 2 + i
                t = k * steps + e
                arrived(t)
                fetch(t + depth - 1)

                @pl.when(k == 0)
                def _():
                    load(e).wait()

                for c in range(0, W, NT):
                    of[i, :, pl.ds(c, NT)] = dot(hv[e], wbuf[t % depth, :, pl.ds(c, NT)])
            at = pl.ds(pl.multiple_of(p * 2 * slots, 16), 2 * slots)
            for b in range(n):
                lines = pl.ds(b * slots, slots)
                o[b, at, :] = jnp.concatenate([of[0, lines, :], of[1, lines, :]], axis=0).astype(BF)

            @pl.when((p == 1) & (k >= 1))
            def _():
                chip_sums(k - 1)

            @pl.when((p == 2) & (k >= 2))
            def _():
                pass_on(k - 2)

            @pl.when((p == 3) & (k >= 4))
            def _():
                complete(k - 4)

        t = k * steps + per
        arrived(t)
        fetch(t + depth - 1)

        @pl.when(k == 0)
        def _():
            load_s.wait()

        @pl.when(k >= 2)
        def _():
            pair(k - 2).wait_send()

        @pl.loop(0, n // 2)
        def _(c):
            psend[k % 2, c] = dot(cm[c * 2 + 1 - core], o[c * 2 + 1 - core]).astype(BF)

        pair(k).start()

        @pl.loop(0, n // 2)
        def _(c):
            keep[c] = dot(cm[c * 2 + core], o[c * 2 + core])

        cols = pl.ds(pl.multiple_of(k * W, W), W)
        tot[:, cols] = dot(hsv[...], wbuf[t % depth])

    chip_sums(chunks - 1)
    pass_on(chunks - 2)
    pass_on(chunks - 1)
    for k in range(chunks - 4, chunks):
        complete(k)
    out(chunks - 2).wait()
    out(chunks - 1).wait()
    for k in range(chunks - 2, chunks):
        pair(k).wait_send()

    @pl.loop(0, chunks)
    def _(k):
        for way in range(2):
            first(k, way).wait_send()
            for part in range(2):
                second(k, way, part).wait_send()


def solution(mesh):
    n = mesh.shape["ep"]

    def body(x, expert, slot, gate, wg, wu, wd, sg, su, sd):
        T, D = x.shape[2:]
        top = expert.shape[3]
        per, _, ff = wg.shape
        slots = 5 * T * top // (4 * per * n)
        rows, chunks = n * slots, D // W
        code = jnp.where(slot < slots, expert * slots + slot, -1).astype(F32)
        rt = jnp.concatenate([code[0, 0].T, gate[0, 0].T], axis=0)
        dma = pltpu.SemaphoreType.DMA
        limit = 67043328
        h, hs, rt_all = pl.pallas_call(
            functools.partial(project, n, slots),
            out_shape=[
                jax.ShapeDtypeStruct((per, rows, ff), BF),
                jax.ShapeDtypeStruct((T, ff), BF),
                jax.ShapeDtypeStruct((n, 2 * top, T), F32),
            ],
            in_specs=[ANY, VM] + [ANY] * 4,
            out_specs=[ANY, ANY, VM],
            scratch_shapes=[
                pltpu.VMEM((chunks, n, T, W), BF),
                pltpu.VMEM((n, per * slots, T), BF),
                pltpu.VMEM((per, rows, 2 * ff), F32),
                pltpu.VMEM((3, W, 2 * ff), BF),
                pltpu.VMEM((2, rows, W), F32),
                pltpu.VMEM((per, rows, W), BF),
                pltpu.VMEM((2, rows, ff), BF),
                dma((chunks,)), dma((3, 2)), dma((2,)),
                dma((n,)), dma((n,)),
                dma((2, 2, chunks)), dma((2, 2, chunks)),
                dma((2, chunks)), dma((2, chunks)),
                dma((5, chunks)), dma((5, chunks)),
            ],
            compiler_params=pltpu.CompilerParams(
                collective_id=0, has_side_effects=True, vmem_limit_bytes=limit),
            name="project",
        )(x[0, 0], rt, sg, su, wg, wu)
        pad = -(-per * slots // 128) * 128
        y = pl.pallas_call(
            functools.partial(finish, n, slots),
            out_shape=jax.ShapeDtypeStruct((T, D), BF),
            in_specs=[ANY, ANY, VM, ANY, ANY],
            out_specs=ANY,
            scratch_shapes=[
                pltpu.VMEM((per, rows, ff), BF),
                pltpu.VMEM((T, ff), BF),
                pltpu.VMEM((n, T, pad), BF),
                pltpu.VMEM((4, ff, W), BF),
                pltpu.VMEM((2, rows, W), F32),
                pltpu.VMEM((n, pad, W), BF),
                pltpu.VMEM((n // 2, T, W), F32),
                pltpu.VMEM((2, n // 2, T, W), BF),
                pltpu.VMEM((chunks, n // 2, T, W), BF),
                pltpu.VMEM((T, D), F32),
                pltpu.VMEM((chunks, 2, T // 2, W), F32),
                pltpu.VMEM((chunks, 2, T // 2, W), BF),
                pltpu.VMEM((chunks, 2, T // 2, W), BF),
                pltpu.VMEM((chunks, 2, T, W), BF),
                pltpu.VMEM((chunks, 2, T, W), BF),
                pltpu.VMEM((2, T, W), BF),
                dma((per + 1,)), dma((4,)), dma((2,)),
                dma((chunks,)), dma((chunks,)),
                dma((2, chunks)), dma((2, chunks)),
                dma((2, 2, chunks)), dma((2, 2, chunks)),
            ],
            compiler_params=pltpu.CompilerParams(
                collective_id=1, has_side_effects=True, vmem_limit_bytes=limit),
            name="finish",
        )(h, hs, rt_all, wd, sd)
        return y[None, None]

    lead = P("dp", "ep", None, None)
    w = P("ep", None, None)
    s = P(None, None)
    return jax.shard_map(
        body, mesh=mesh, in_specs=(lead,) * 4 + (w,) * 3 + (s,) * 3, out_specs=lead, check_vma=False
    )
```

time: 677 us -> 235 us (0.35)
  blocking collectives: 238 us -> 0 us
  Pallas kernels: 0 us -> 230 us
  matrix products: 205 us -> 0 us
  waiting for transfers between devices: 195 us -> 0 us
  local copies, waits for them, and re-layouts: 31.3 us -> 3.13 us
    another operation x1 -> x0, blocking collectives: 238 us -> none  [placed(): return lax.with_sharding_constraint(v, NamedSharding(mesh, P(*spec)))]
    pallas_call x0 -> x2, Pallas kernels: none -> 230 us  [the longest x1 134 us: body(): pl.pallas_call(functools.partial(project, n, slots), out_shape=[jax.Shape...]
    dot_general x9 -> x0, matrix products: 205 us -> none  [einsum(): return jnp.einsum(form, a.astype(jnp.float32), b.astype(jnp.float32))]
    another operation x1 -> x0, waiting for transfers between devices: 195 us -> none  [placed(): return lax.with_sharding_constraint(v, NamedSharding(mesh, P(*spec)))]
    another operation x1 -> x0, local copies, waits for them, and re-layouts: 17.5 us -> none  [placed(): return lax.with_sharding_constraint(v, NamedSharding(mesh, P(*spec)))]
    convert_element_type x3 -> x0, local copies, waits for them, and re-layouts: 11.4 us -> none  [the longest x1 5.62 us: step(): einsum('abtke,abtkc->abtec', to_expert, to_slot).astype(jnp.bfloat16)]
  transfers between devices with their start and end apart: 1 -> 0, of which waited for: 1 -> 0; matrix products, arithmetic and copies ran while one was open for 5% -> 0% of each run, Pallas kernels for 0% -> 0%
where the time goes in v1:
time: 235 us
  Pallas kernels  230 us (98%)
  local copies, waits for them, and re-layouts  3.13 us (1%)
    pallas_call x1, Pallas kernels, body(): pl.pallas_call(functools.partial(project, n, slots), out_shape=[jax.Shape...  134 us
    pallas_call x1, Pallas kernels, body(): pl.pallas_call(functools.partial(finish, n, slots), out_shape=jax.ShapeDt...  96.2 us

profile of v1, /device:TPU:112, one launch (start us, length us, event | category | flops | bytes accessed | tf_op | source)
XLA Modules:
  0.0 235.0 jit_solution(691407749350279070)
XLA Ops:
  0.0 0.7 convert_bitcast_fusion
  0.7 1.3 pad_maximum_fusion.rt
  2.0 133.7 %project.1 = (bf16[8,320,1408]{2,1,0:T(8,128)(2,1)}, bf16[256,1408]{1,0:T(8,128)(2,1)}, f32[8,16,256]{2,1,0:T(8,128)}) custom-call(bf16[256,4096]{1,0:T(8,128)(2,1)} %bitcast.10, f32[16,256]{1,0:T(8,128)} %pad_maximum_fusion.rt, bf16[4096,1408]{1,0:T(8,128)(2,1)} %sg.1, bf16[4096,1408]{1,0:T(8,128)(2,1)} %su.1, bf16[8,4096,1408]{2,1,0:T(8,128)(2,1)} %wg.1, ...), custom_call_target="tpu_custom_call" | custom-call | tf_op jit(solution)/shard_map/project/pallas_call | solution.py:450
  135.7 96.2 %finish.1 = bf16[256,4096]{1,0:T(8,128)(2,1)} custom-call(bf16[8,320,1408]{2,1,0:T(8,128)(2,1)} %get-tuple-element.8.h, bf16[256,1408]{1,0:T(8,128)(2,1)} %get-tuple-element.9.hs, f32[8,16,256]{2,1,0:T(8,128)} %get-tuple-element.10.rt_all, bf16[8,1408,4096]{2,1,0:T(8,128)(2,1)} %wd.1, bf16[1408,4096]{1,0:T(8,128)(2,1)} %sd.1), custom_call_target="tpu_custom_call" | custom-call | tf_op jit(solution)/shard_map/finish/pallas_call | solution.py:478
  231.9 3.1 %copy.12 = bf16[1,1,256,4096]{3,2,1,0:T(8,128)(2,1)} copy(bf16[1,1,256,4096]{3,2,1,0:T(8,128)(2,1)} %bitcast.9) | data formatting | bytes 4194304

commit v2 on v1

--- a/solution.py
+++ b/solution.py
@@ -10,13 +10,16 @@
 MESH = pl.DeviceIdType.MESH
 BF, F32 = jnp.bfloat16, jnp.float32
 ANY = pl.BlockSpec(memory_space=pl.ANY)
-VM = pl.BlockSpec(memory_space=pltpu.VMEM)
 W = 512
 NT = 256
 
 
 def dot(a, b):
     return jnp.dot(a, b, preferred_element_type=F32)
+
+
+def silu(v):
+    return 0.5 * v * (1.0 + jnp.tanh(0.5 * v))
 
 
 def remote(src, dst, send, recv, to):
@@ -40,8 +43,8 @@
     pl.semaphore_wait(barrier, n - 1)
 
 
-def project(n, slots, x, rt, sg, su, wg, wu, h_out, hs_out, rt_all,
-            xg, oh, acc, wbuf, zf, z, hst, lsem, wsem, hsem, rts, rtr, own_s, own_r, fwd_s, fwd_r, par_s, par_r):
+def project(n, slots, x, rt, sg, su, wg, wu, h_out, hs_out, rt_out,
+            rt_all, xg, oh, acc, wbuf, z, hst, lsem, wsem, hsem, rts, rtr, own_s, own_r, fwd_s, fwd_r, par_s, par_r):
     per, _, ff = wg.shape
     T, D = x.shape
     half, rows, chunks = T // 2, n * slots, D // W
@@ -106,7 +109,8 @@
         own(k, 1, 0).start()
         par(k, 0).start()
 
-    rt_all[me] = rt[...]
+    mine_in = pltpu.make_async_copy(rt, rt_all.at[me], rts.at[0])
+    mine_in.start()
     greet(n, me)
     local(0).wait()
     send_own(0)
@@ -123,6 +127,7 @@
         def _():
             send_own(k + 1)
 
+    def across(k):
         own(k, 0, 1).wait_recv()
         par(k, 1).start()
         own(k, 1, 0).wait_recv()
@@ -135,11 +140,15 @@
         par(k, 4).start()
 
     def service(g, e):
-        @pl.when((e == 4) & (g < chunks))
+        @pl.when(e == 1)
         def _():
             near(g)
 
-        @pl.when((e == per - 1) & (g < chunks))
+        @pl.when(e == 3)
+        def _():
+            across(g)
+
+        @pl.when(e == per - 2)
         def _():
             far(g)
 
@@ -147,18 +156,21 @@
         width = 2 * ff
         for c in range(0, width, NT):
             cols = pl.ds(c, min(NT, width - c))
-            old = acc[e, pl.ds(0, n_rows), cols]
-            acc[e, pl.ds(0, n_rows), cols] = jnp.where(first, 0.0, old) + dot(lhs, wbuf[slot, :, cols])
-
-    def act(e, hslot, n_rows):
-        step = 32
-
-        @pl.loop(0, n_rows // step)
-        def _(r):
-            at = pl.ds(pl.multiple_of(r * step, step), step)
-            g = acc[e, at, pl.ds(0, ff)]
-            u = acc[e, at, pl.ds(ff, ff)]
-            hst[hslot, at, :] = (jax.nn.silu(g) * u).astype(BF)
+            lone = width - c <= NT and (width // NT) % 2 == 1
+            step = n_rows // 2 if lone else n_rows
+            for r in range(0, n_rows, step):
+                at = pl.ds(r, step)
+                part = dot(lhs[r:r + step], wbuf[slot, :, cols])
+                acc[e, at, cols] = jnp.where(first, 0.0, acc[e, at, cols]) + part
+
+    def gate_up_act(e, lhs, slot, hslot, n_rows):
+        at = pl.ds(0, n_rows)
+        for c in range(0, ff, NT):
+            g_cols = pl.ds(c, min(NT, ff - c))
+            u_cols = pl.ds(ff + c, min(NT, ff - c))
+            g = acc[e, at, g_cols] + dot(lhs, wbuf[slot, :, g_cols])
+            u = acc[e, at, u_cols] + dot(lhs, wbuf[slot, :, u_cols])
+            hst[hslot, at, g_cols] = (silu(g) * u).astype(BF)
 
     def shared_out():
         return pltpu.make_async_copy(hst.at[0, pl.ds(0, T)], hs_out, hsem.at[0])
@@ -166,7 +178,7 @@
     def expert_out(e):
         return pltpu.make_async_copy(hst.at[e % 2], h_out.at[e], hsem.at[e % 2])
 
-    @pl.loop(0, chunks)
+    @pl.loop(0, chunks - 1)
     def _(t):
         arrived(t)
         fetch(t + 2)
@@ -176,13 +188,24 @@
             local(t).wait()
 
         gate_up(0, xg[t, me], t % 3, t == 0, T)
-        service(0, t)
-
-    act(0, 0, T)
+
+        @pl.when(t == 3)
+        def _():
+            near(0)
+
+    last = chunks - 1
+    arrived(last)
+    fetch(last + 2)
+    local(last).wait()
+    gate_up_act(0, xg[last, me], last % 3, 0, T)
+    across(0)
     shared_out().start()
 
     for off in range(1, n):
         remote(rt, rt_all.at[me], rts.at[off], rtr.at[off], (me + off) % n).wait()
+    mine_in.wait()
+    tables = pltpu.make_async_copy(rt_all, rt_out, rts.at[0])
+    tables.start()
 
     @pl.loop(0, n)
     def _(b):
@@ -193,43 +216,48 @@
             hit = jnp.where(codes[j:j + 1, :] == row, 1.0, hit)
         oh[b] = hit.astype(BF)
 
-    @pl.loop(0, chunks)
-    def _(k):
+    far(0)
+
+    def dispatch(k):
         for i in range(5):
             par(k, i).wait_recv()
-
-        @pl.loop(0, n // 2)
-        def _(p):
-            for i in range(2):
-                b = p * 2 + i
-                for c in range(0, W, NT):
-                    zf[i, :, pl.ds(c, NT)] = dot(oh[b], xg[k, b, :, pl.ds(c, NT)])
-            at = pl.ds(pl.multiple_of(p * 2 * slots, 16), 2 * slots)
-            for e in range(per):
-                lines = pl.ds(e * slots, slots)
-                z[e, at, :] = jnp.concatenate([zf[0, lines, :], zf[1, lines, :]], axis=0).astype(BF)
+        for p in range(n // 2):
+            at = pl.ds(p * 2 * slots, 2 * slots)
+            for c in range(0, W, NT):
+                cols = pl.ds(c, NT)
+                two = [dot(oh[b], xg[k, b, :, cols]) for b in (p * 2, p * 2 + 1)]
+                for e in range(per):
+                    z[e, at, cols] = jnp.concatenate([v[e * slots:(e + 1) * slots] for v in two], axis=0).astype(BF)
+
+    @pl.loop(0, last)
+    def _(k):
+        dispatch(k)
 
         @pl.loop(0, per)
         def _(e):
             t = chunks + k * per + e
             arrived(t)
             fetch(t + 2)
+            service(k + 1, e)
             gate_up(e, z[e], t % 3, k == 0, rows)
-            service(k + 1, e)
-
-            @pl.when(k == chunks - 1)
-            def _():
-                @pl.when(e == 0)
-                def _():
-                    shared_out().wait()
-
-                @pl.when(e >= 2)
-                def _():
-                    expert_out(e - 2).wait()
-
-                act(e, e % 2, rows)
-                expert_out(e).start()
-
+
+    dispatch(last)
+    shared_out().wait()
+
+    @pl.loop(0, per)
+    def _(e):
+        t = chunks + last * per + e
+        arrived(t)
+        fetch(t + 2)
+
+        @pl.when(e >= 2)
+        def _():
+            expert_out(e - 2).wait()
+
+        gate_up_act(e, z[e], t % 3, e % 2, rows)
+        expert_out(e).start()
+
+    tables.wait()
     expert_out(per - 2).wait()
     expert_out(per - 1).wait()
 
@@ -243,8 +271,8 @@
             par(k, i).wait_send()
 
 
-def finish(n, slots, h, hs, rt_all, wd, sd, y,
-           hv, hsv, cm, wbuf, of, o, keep, psend, precv, tot, s3, s1s, s1r, s3s, s3r, yb,
+def finish(n, slots, h, hs, rt_in, wd, sd, y,
+           rt_all, hv, hsv, cm, wbuf, o, keep, psend, precv, tot, s3, s1s, s1r, s3s, s3r, yb,
            hsem, wsem, ysem, par_s, par_r, s1_s, s1_r, s3_s, s3_r):
     per, ff, D = wd.shape
     T = hs.shape[0]
@@ -280,6 +308,8 @@
         return pltpu.make_async_copy(h.at[e], hv.at[e], hsem.at[e])
 
     load_s = pltpu.make_async_copy(hs, hsv, hsem.at[per])
+    tables = pltpu.make_async_copy(rt_in, rt_all, hsem.at[per + 1])
+    tables.start()
     load(0).start()
     fetch(0)
     load(1).start()
@@ -287,10 +317,11 @@
     for e in range(2, per):
         load(e).start()
     load_s.start()
-    for t in range(2, depth - 1):
+    for t in range(2, 4):
         fetch(t)
 
     pad = o.shape[1]
+    tables.wait()
 
     @pl.loop(0, n)
     def _(b):
@@ -362,38 +393,37 @@
     def _(k):
         @pl.loop(0, per // 2)
         def _(p):
+            t = k * steps + p * 2
             for i in range(2):
-                e = p * 2 + i
-                t = k * steps + e
-                arrived(t)
-                fetch(t + depth - 1)
+                arrived(t + i)
+                fetch(t + 4 + i)
 
                 @pl.when(k == 0)
                 def _():
-                    load(e).wait()
-
-                for c in range(0, W, NT):
-                    of[i, :, pl.ds(c, NT)] = dot(hv[e], wbuf[t % depth, :, pl.ds(c, NT)])
+                    load(p * 2 + i).wait()
+
             at = pl.ds(pl.multiple_of(p * 2 * slots, 16), 2 * slots)
-            for b in range(n):
-                lines = pl.ds(b * slots, slots)
-                o[b, at, :] = jnp.concatenate([of[0, lines, :], of[1, lines, :]], axis=0).astype(BF)
-
-            @pl.when((p == 1) & (k >= 1))
+            for c in range(0, W, NT):
+                cols = pl.ds(c, NT)
+                two = [dot(hv[p * 2 + i], wbuf[(t + i) % depth, :, cols]) for i in range(2)]
+                for b in range(n):
+                    o[b, at, cols] = jnp.concatenate([v[b * slots:(b + 1) * slots] for v in two], axis=0).astype(BF)
+
+            @pl.when((p == 0) & (k >= 1))
             def _():
                 chip_sums(k - 1)
 
-            @pl.when((p == 2) & (k >= 2))
+            @pl.when((p == 1) & (k >= 2))
             def _():
                 pass_on(k - 2)
 
-            @pl.when((p == 3) & (k >= 4))
+            @pl.when((p == 2) & (k >= 4))
             def _():
                 complete(k - 4)
 
         t = k * steps + per
         arrived(t)
-        fetch(t + depth - 1)
+        fetch(t + 4)
 
         @pl.when(k == 0)
         def _():
@@ -403,16 +433,13 @@
         def _():
             pair(k - 2).wait_send()
 
-        @pl.loop(0, n // 2)
-        def _(c):
-            psend[k % 2, c] = dot(cm[c * 2 + 1 - core], o[c * 2 + 1 - core]).astype(BF)
-
+        for c in range(n // 2):
+            b = c * 2 + 1 - core
+            psend[k % 2, c] = dot(cm[b], o[b]).astype(BF)
         pair(k).start()
-
-        @pl.loop(0, n // 2)
-        def _(c):
-            keep[c] = dot(cm[c * 2 + core], o[c * 2 + core])
-
+        for c in range(n // 2):
+            b = c * 2 + core
+            keep[c] = dot(cm[b], o[b])
         cols = pl.ds(pl.multiple_of(k * W, W), W)
         tot[:, cols] = dot(hsv[...], wbuf[t % depth])
 
@@ -454,14 +481,14 @@
                 jax.ShapeDtypeStruct((T, ff), BF),
                 jax.ShapeDtypeStruct((n, 2 * top, T), F32),
             ],
-            in_specs=[ANY, VM] + [ANY] * 4,
-            out_specs=[ANY, ANY, VM],
+            in_specs=[ANY] * 6,
+            out_specs=[ANY] * 3,
             scratch_shapes=[
+                pltpu.VMEM((n, 2 * top, T), F32),
                 pltpu.VMEM((chunks, n, T, W), BF),
                 pltpu.VMEM((n, per * slots, T), BF),
                 pltpu.VMEM((per, rows, 2 * ff), F32),
                 pltpu.VMEM((3, W, 2 * ff), BF),
-                pltpu.VMEM((2, rows, W), F32),
                 pltpu.VMEM((per, rows, W), BF),
                 pltpu.VMEM((2, rows, ff), BF),
                 dma((chunks,)), dma((3, 2)), dma((2,)),
@@ -478,14 +505,14 @@
         y = pl.pallas_call(
             functools.partial(finish, n, slots),
             out_shape=jax.ShapeDtypeStruct((T, D), BF),
-            in_specs=[ANY, ANY, VM, ANY, ANY],
+            in_specs=[ANY] * 5,
             out_specs=ANY,
             scratch_shapes=[
+                pltpu.VMEM((n, 2 * top, T), F32),
                 pltpu.VMEM((per, rows, ff), BF),
                 pltpu.VMEM((T, ff), BF),
                 pltpu.VMEM((n, T, pad), BF),
-                pltpu.VMEM((4, ff, W), BF),
-                pltpu.VMEM((2, rows, W), F32),
+                pltpu.VMEM((6, ff, W), BF),
                 pltpu.VMEM((n, pad, W), BF),
                 pltpu.VMEM((n // 2, T, W), F32),
                 pltpu.VMEM((2, n // 2, T, W), BF),
@@ -497,7 +524,7 @@
                 pltpu.VMEM((chunks, 2, T, W), BF),
                 pltpu.VMEM((chunks, 2, T, W), BF),
                 pltpu.VMEM((2, T, W), BF),
-                dma((per + 1,)), dma((4,)), dma((2,)),
+                dma((per + 2,)), dma((6,)), dma((2,)),
                 dma((chunks,)), dma((chunks,)),
                 dma((2, chunks)), dma((2, chunks)),
                 dma((2, 2, chunks)), dma((2, 2, chunks)),

time: 235 us -> 196 us (0.83)
  Pallas kernels: 230 us -> 191 us
    pallas_call x1, Pallas kernels: 134 us -> 104 us  [body(): pl.pallas_call(functools.partial(project, n, slots), out_shape=[jax.Shape...]
    pallas_call x1, Pallas kernels: 96.2 us -> 87.2 us  [body(): pl.pallas_call(functools.partial(finish, n, slots), out_shape=jax.ShapeDt...]
where the time goes in v2:
time: 196 us
  Pallas kernels  191 us (97%)
  local copies, waits for them, and re-layouts  3.13 us (2%)
  other arithmetic  2.02 us (1%)
    pallas_call x1, Pallas kernels, body(): pl.pallas_call(functools.partial(project, n, slots), out_shape=[jax.Shape...  104 us
    pallas_call x1, Pallas kernels, body(): pl.pallas_call(functools.partial(finish, n, slots), out_shape=jax.ShapeDt...  87.2 us

profile of v2, /device:TPU:112, one launch (start us, length us, event | category | flops | bytes accessed | tf_op | source)
XLA Modules:
  0.0 196.2 jit_solution(1874464799897068393)
XLA Ops:
  0.0 0.7 convert_bitcast_fusion
  0.7 1.3 pad_maximum_fusion.rt
  2.0 103.8 %project.1 = (bf16[8,320,1408]{2,1,0:T(8,128)(2,1)}, bf16[256,1408]{1,0:T(8,128)(2,1)}, f32[8,16,256]{2,1,0:T(8,128)}) custom-call(bf16[256,4096]{1,0:T(8,128)(2,1)} %bitcast.10, f32[16,256]{1,0:T(8,128)} %pad_maximum_fusion.rt, bf16[4096,1408]{1,0:T(8,128)(2,1)} %sg.1, bf16[4096,1408]{1,0:T(8,128)(2,1)} %su.1, bf16[8,4096,1408]{2,1,0:T(8,128)(2,1)} %wg.1, ...), custom_call_target="tpu_custom_call" | custom-call | tf_op jit(solution)/shard_map/project/pallas_call | solution.py:477
  105.8 87.2 %finish.1 = bf16[256,4096]{1,0:T(8,128)(2,1)} custom-call(bf16[8,320,1408]{2,1,0:T(8,128)(2,1)} %get-tuple-element.8.h, bf16[256,1408]{1,0:T(8,128)(2,1)} %get-tuple-element.9.hs, f32[8,16,256]{2,1,0:T(8,128)} %get-tuple-element.10.rt_in, bf16[8,1408,4096]{2,1,0:T(8,128)(2,1)} %wd.1, bf16[1408,4096]{1,0:T(8,128)(2,1)} %sd.1), custom_call_target="tpu_custom_call" | custom-call | tf_op jit(solution)/shard_map/finish/pallas_call | solution.py:505
  193.0 3.1 %copy.12 = bf16[1,1,256,4096]{3,2,1,0:T(8,128)(2,1)} copy(bf16[1,1,256,4096]{3,2,1,0:T(8,128)(2,1)} %bitcast.9) | data formatting | bytes 4194304

commit v3 on v2

--- a/solution.py
+++ b/solution.py
@@ -343,9 +343,8 @@
     def first(k, way):
         return remote(s1s.at[k, way], s1r.at[k, way], s1_s.at[way, k], s1_r.at[way, k], (right, left)[way])
 
-    def second(k, way, part):
-        return remote(s3s.at[k, way, parts[part]], s3r.at[k, way, parts[part]],
-                      s3_s.at[way, part, k], s3_r.at[way, part, k], (right, left)[way])
+    def second(k, way):
+        return remote(s3s.at[k, way], s3r.at[k, way], s3_s.at[way, k], s3_r.at[way, k], (right, left)[way])
 
     def chip_sums(k):
         pair(k).wait_recv()
@@ -356,12 +355,9 @@
             return keep[c, parts[part], :] + precv[k, c, parts[part], :].astype(F32)
 
         for way in range(2):
-            s1s[k, way] = both(2, way).astype(BF)
+            s1s[k, way, 0] = both(2, way).astype(BF)
+            s1s[k, way, 1] = both((1, 3)[way], 1 - way).astype(BF)
             first(k, way).start()
-        for way in range(2):
-            far = 1 - way
-            s3s[k, way, parts[far], :] = both((1, 3)[way], far).astype(BF)
-            second(k, way, far).start()
         for way in range(2):
             s3[k, way] = both((1, 3)[way], way)
         for part in range(2):
@@ -370,23 +366,24 @@
     def pass_on(k):
         for way in range(2):
             first(k, way).wait_recv()
-            s3s[k, way, parts[way], :] = (s3[k, way] + s1r[k, way].astype(F32)).astype(BF)
-            second(k, way, way).start()
+            s3s[k, way] = (s3[k, way] + s1r[k, way, 0].astype(F32)).astype(BF)
+            second(k, way).start()
 
     def out(k):
         return pltpu.make_async_copy(yb.at[k % 2], y.at[:, pl.ds(k * W, W)], ysem.at[k % 2])
 
     def complete(k):
         for way in range(2):
-            for part in range(2):
-                second(k, way, part).wait_recv()
+            second(k, way).wait_recv()
 
         @pl.when(k >= 2)
         def _():
             out(k - 2).wait()
 
         cols = pl.ds(pl.multiple_of(k * W, W), W)
-        yb[k % 2] = (tot[:, cols] + s3r[k, 0].astype(F32) + s3r[k, 1].astype(F32)).astype(BF)
+        for way in range(2):
+            sums = tot[parts[way], cols] + s3r[k, way].astype(F32)
+            yb[k % 2, parts[way], :] = (sums + s1r[k, 1 - way, 1].astype(F32)).astype(BF)
         out(k).start()
 
     @pl.loop(0, chunks)
@@ -457,8 +454,7 @@
     def _(k):
         for way in range(2):
             first(k, way).wait_send()
-            for part in range(2):
-                second(k, way, part).wait_send()
+            second(k, way).wait_send()
 
 
 def solution(mesh):
@@ -519,15 +515,15 @@
                 pltpu.VMEM((chunks, n // 2, T, W), BF),
                 pltpu.VMEM((T, D), F32),
                 pltpu.VMEM((chunks, 2, T // 2, W), F32),
+                pltpu.VMEM((chunks, 2, 2, T // 2, W), BF),
+                pltpu.VMEM((chunks, 2, 2, T // 2, W), BF),
                 pltpu.VMEM((chunks, 2, T // 2, W), BF),
                 pltpu.VMEM((chunks, 2, T // 2, W), BF),
-                pltpu.VMEM((chunks, 2, T, W), BF),
-                pltpu.VMEM((chunks, 2, T, W), BF),
                 pltpu.VMEM((2, T, W), BF),
                 dma((per + 2,)), dma((6,)), dma((2,)),
                 dma((chunks,)), dma((chunks,)),
                 dma((2, chunks)), dma((2, chunks)),
-                dma((2, 2, chunks)), dma((2, 2, chunks)),
+                dma((2, chunks)), dma((2, chunks)),
             ],
             compiler_params=pltpu.CompilerParams(
                 collective_id=1, has_side_effects=True, vmem_limit_bytes=limit),

time: 196 us -> 196 us (level)
  no operation moved by 1% of the time
where the time goes in v3:
time: 196 us
  Pallas kernels  191 us (97%)
  local copies, waits for them, and re-layouts  3.13 us (2%)
  other arithmetic  2.02 us (1%)
    pallas_call x1, Pallas kernels, body(): pl.pallas_call(functools.partial(project, n, slots), out_shape=[jax.Shape...  104 us
    pallas_call x1, Pallas kernels, body(): pl.pallas_call(functools.partial(finish, n, slots), out_shape=jax.ShapeDt...  86.9 us

profile of v3, /device:TPU:112, one launch (start us, length us, event | category | flops | bytes accessed | tf_op | source)
XLA Modules:
  0.0 195.8 jit_solution(11034001828186350074)
XLA Ops:
  0.0 0.7 convert_bitcast_fusion
  0.7 1.3 pad_maximum_fusion.rt
  2.0 103.8 %project.1 = (bf16[8,320,1408]{2,1,0:T(8,128)(2,1)}, bf16[256,1408]{1,0:T(8,128)(2,1)}, f32[8,16,256]{2,1,0:T(8,128)}) custom-call(bf16[256,4096]{1,0:T(8,128)(2,1)} %bitcast.10, f32[16,256]{1,0:T(8,128)} %pad_maximum_fusion.rt, bf16[4096,1408]{1,0:T(8,128)(2,1)} %sg.1, bf16[4096,1408]{1,0:T(8,128)(2,1)} %su.1, bf16[8,4096,1408]{2,1,0:T(8,128)(2,1)} %wg.1, ...), custom_call_target="tpu_custom_call" | custom-call | tf_op jit(solution)/shard_map/project/pallas_call | solution.py:473
  105.8 86.9 %finish.1 = bf16[256,4096]{1,0:T(8,128)(2,1)} custom-call(bf16[8,320,1408]{2,1,0:T(8,128)(2,1)} %get-tuple-element.8.h, bf16[256,1408]{1,0:T(8,128)(2,1)} %get-tuple-element.9.hs, f32[8,16,256]{2,1,0:T(8,128)} %get-tuple-element.10.rt_in, bf16[8,1408,4096]{2,1,0:T(8,128)(2,1)} %wd.1, bf16[1408,4096]{1,0:T(8,128)(2,1)} %sd.1), custom_call_target="tpu_custom_call" | custom-call | tf_op jit(solution)/shard_map/finish/pallas_call | solution.py:501
  192.7 3.1 %copy.12 = bf16[1,1,256,4096]{3,2,1,0:T(8,128)(2,1)} copy(bf16[1,1,256,4096]{3,2,1,0:T(8,128)(2,1)} %bitcast.9) | data formatting | bytes 4194304
